TPU v7x, 256 devices: a whole 4x4x8 slice. The times are simulated.
256 devices in a mesh: dp: 16 (over z, x_lo), tp: 16 (over y, x_hi, core).
Axes of the slice: x: 4 (x_hi: 2, x_lo: 2; x = x_hi * 2 + x_lo), y: 4, z: 8, core: 2. Of those that a mesh axis runs over, the one named last changes fastest.
Arguments:
- queries: bfloat16 [8192, 8192], P('dp', 'tp'), parts along dimension 0, may hold values from -200 to 200
- new_keys: bfloat16 [8192, 1024], P('dp', 'tp'), parts along dimension 0, may hold values from -9 to 9
- new_values: bfloat16 [8192, 1024], P('dp', 'tp'), parts along dimension 0, may hold values from -60 to 60
- cache_keys: bfloat16 [64, 32768, 128], P('dp', 'tp'), parts along dimension 0, may hold values from -4 to 4
- cache_values: bfloat16 [64, 32768, 128], P('dp', 'tp'), parts along dimension 0, may hold values from -60 to 60
- out_weight: bfloat16 [8192, 8192], P('tp'), may hold values from -0.09375 to 0.09375
- residual: bfloat16 [8192, 8192], P('dp', 'tp'), parts along dimension 0, may hold values from -8 to 8
- norm_gain: bfloat16 [8192], P('tp'), may hold values from 0.5 to 1.5
Outputs:
- normed: bfloat16 [8192, 8192], P('dp', 'tp'), parts along dimension 0
There are 16 independent parts, one for each index of `dp`. A program takes and returns all parts, laid end to end along the dimension named above; an argument that names none is the same for every part. Nothing has to cross between parts.
All inputs are finite; a program needn't handle non-finite values.
Results may differ from a plain program's by a relative error of at most 0.015.
Values may be sent and summed in bfloat16 or wider, within the bound.
A program may use at most 128 MiB of HBM per device.

v0:
```python
import jax
import jax.numpy as jnp
from jax import lax
from jax.sharding import PartitionSpec as P

D = 8192
HD = 128
SPAN = 128
SEQS = 4


EPSILON = 1e-05


def partner(value, axis, bit):
    mask = 2**bit
    pairs = [(source, source ^ mask) for source in range(lax.axis_size(axis))]
    return lax.ppermute(value, axis, pairs)


def sent_to_all(shard, axis):
    copies = jnp.broadcast_to(shard, (lax.axis_size(axis), *shard.shape))
    return lax.all_to_all(copies, axis, split_axis=0, concat_axis=0, tiled=True)


def of_everyone(shard, axis):
    return sent_to_all(shard, axis).sum(axis=0)


def attend_block(query_rows, stored_keys, stored_values, fresh_keys, fresh_values, local_kv):
    heads_here = query_rows.shape[1] // HD
    groups = heads_here // local_kv
    length = stored_keys.shape[1] // local_kv
    scaling = HD ** (-0.5)
    grouped = query_rows.reshape(SEQS, SPAN, local_kv, groups, HD)
    old_keys = stored_keys.reshape(SEQS, local_kv, length, HD)
    old_values = stored_values.reshape(SEQS, local_kv, length, HD)
    scores = (
        jnp.einsum("sighd,sgjd->sghij", grouped, old_keys, preferred_element_type=jnp.float32)
        * scaling
    )
    peak = jnp.max(scores, axis=-1)
    recent_keys = fresh_keys.reshape(SEQS, SPAN, local_kv, HD)
    recent_values = fresh_values.reshape(SEQS, SPAN, local_kv, HD)
    recent_scores = (
        jnp.einsum("sighd,sjgd->sghij", grouped, recent_keys, preferred_element_type=jnp.float32)
        * scaling
    )
    causal = jnp.arange(SPAN)[:, None] >= jnp.arange(SPAN)[None, :]
    recent_scores = jnp.where(causal, recent_scores, -jnp.inf)
    peak = jnp.maximum(peak, jnp.max(recent_scores, axis=-1))
    weights = jnp.exp(scores - peak[..., None])
    total = jnp.sum(weights, axis=-1)
    mixed = jnp.einsum(
        "sghij,sgjd->sighd",
        weights.astype(jnp.bfloat16),
        old_values,
        preferred_element_type=jnp.float32,
    )
    recent_weights = jnp.exp(recent_scores - peak[..., None])
    total = total + jnp.sum(recent_weights, axis=-1)
    mixed = mixed + jnp.einsum(
        "sghij,sjgd->sighd",
        recent_weights.astype(jnp.bfloat16),
        recent_values,
        preferred_element_type=jnp.float32,
    )
    return (mixed, peak, total)


def token_layout(stat):
    return jnp.transpose(stat, (0, 3, 1, 2))[..., None]


def finish_rows(mixed, total):
    result = mixed / token_layout(total)
    return result.reshape(SEQS * SPAN, -1).astype(jnp.bfloat16)


def per_device(
    queries, new_keys, new_values, cache_keys, cache_values, out_weight, residual, norm_gain
):
    local_kv = 1
    parity = lax.axis_index("tp") % 2

    def join_dims(own_piece, other_piece):
        first = jnp.concatenate([own_piece, other_piece], axis=-1)
        second = jnp.concatenate([other_piece, own_piece], axis=-1)
        return jnp.where(parity == 0, first, second)

    other_keys, other_values, other_stored_keys, other_stored_values = partner(
        (new_keys, new_values, cache_keys, cache_values), "tp", 0
    )
    fresh_keys = join_dims(new_keys, other_keys)
    fresh_values = join_dims(new_values, other_values)
    stored_keys = jnp.concatenate([cache_keys, other_stored_keys], axis=1)
    stored_values = jnp.concatenate([cache_values, other_stored_values], axis=1)
    mixed, peak, total = attend_block(
        queries, stored_keys, stored_values, fresh_keys, fresh_values, local_kv
    )
    attended = finish_rows(mixed, total)
    projected = lax.psum_scatter(
        lax.dot_general(
            out_weight, attended, (((0,), (1,)), ((), ())), preferred_element_type=jnp.float32
        ).astype(jnp.bfloat16),
        "tp",
        scatter_dimension=0,
        tiled=True,
    ).astype(jnp.float32)
    hidden = residual.astype(jnp.float32) + jnp.transpose(projected)
    squares = of_everyone(jnp.sum(hidden * hidden, axis=1), "tp")
    scaled = (
        hidden * lax.rsqrt(squares / D + EPSILON)[:, None] * norm_gain.astype(jnp.float32)[None, :]
    )
    return scaled.astype(jnp.bfloat16)


def solution(mesh):
    in_specs = (
        P("dp", "tp"),
        P("dp", "tp"),
        P("dp", "tp"),
        P("dp", "tp", None),
        P("dp", "tp", None),
        P("tp", None),
        P("dp", "tp"),
        P("tp"),
    )
    out_specs = P("dp", "tp")
    return jax.shard_map(
        per_device, mesh=mesh, in_specs=in_specs, out_specs=out_specs, check_vma=False
    )
```

profile of v0, /device:TPU:1, one launch (start us, length us, event | category | flops | bytes accessed | tf_op | source)
XLA Modules:
  0.0 206.3 jit_solution(14784281957386837009)
XLA Ops:
  6.5 3.2 %collective-permute-start.1 = (bf16[4,2048,128]{2,1,0:T(8,128)(2,1)}, bf16[4,2048,128]{2,1,0:T(8,128)(2,1)}, u32[]{:S(2)}, u32[]{:S(2)}) collective-permute-start(bf16[4,2048,128]{2,1,0:T(8,128)(2,1)} %param.11), channel_id=1, source_target_pairs={{0,1},{1,0},{2,3},{3,2},{4,5},{5,4},{6,7},{7,6},{8,9},{9,8},{10,11... | collective-permute-start | bytes 6291464 | tf_op jit(solution)/shard_map/ppermute | solution.py:18
  9.7 0.5 collective-permute-start.3
  10.2 2.9 %copy.57 = bf16[4,2048,128]{1,2,0:T(8,128)(2,1)S(1)} copy(bf16[4,2048,128]{2,1,0:T(8,128)(2,1)} %param.12) | data formatting | bytes 4194304 | tf_op args[4]
  13.2 0.3 collective-permute-start
  13.5 1.2 reshape.102
  14.7 0.9 copy_bitcast_fusion.3
  15.5 0.9 copy_bitcast_fusion.1
  16.4 0.0 collective-permute-done.2
  16.4 0.0 collective-permute-done.3
  16.5 0.4 fusion.57
  16.8 15.4 %bitcast_reduce_fusion = (f32[4,4,128]{2,1,0:T(4,128)S(1)}, f32[4,4096,128,4]{2,1,3,0:T(8,128)}) fusion(bf16[4,128,4,128]{3,2,1,0:T(4,128)(2,1)S(1)} %reshape.102, bf16[4,2048,128]{2,1,0:T(8,128)(2,1)} %collective-permute-done.1, bf16[4,2048,128]{2,1,0:T(8,128)(2,1)} %param.11), kind=kOutput, calls=%fused_computation.1 | convolution fusion | flops 2172647424 | bytes 38281216 | tf_op jit(solution)/shard_map/sighd,sgjd->sghij/dot_general | solution.py:39
  32.2 0.2 fusion.26
  32.4 13.6 %fusion.1 = f32[4,4,128]{2,1,0:T(4,128)S(1)} fusion(f32[4,4096,128,4]{2,1,3,0:T(8,128)} %get-tuple-element.6, f32[4,4,128]{2,1,0:T(4,128)S(1)} %max.9), kind=kLoop, calls=%fused_computation.3 | loop fusion | flops 25163776 | bytes 33570816 | tf_op jit(solution)/shard_map/reduce_sum | solution.py:53
  46.0 0.3 fusion.29
  46.3 14.9 %fusion.23 = bf16[4,128,1,4,128]{1,4,3,0,2:T(8,128)(2,1)} fusion(f32[4,128,4,128]{3,1,2,0:T(8,128)S(1)} %fusion.29, f32[4,4096,128,4]{2,1,3,0:T(8,128)} %get-tuple-element.6, f32[4,4,128]{2,1,0:T(4,128)S(1)} %max.9, bf16[4,2048,128]{1,2,0:T(8,128)(2,1)} %collective-permute-done, bf16[4,2048,128]{1,2,0:T(8,128)(2,1)S(1)} %copy.57, ...), kind=kOutput, calls=%fused_computation.22 | convolution fusion | flops 2181824512 | bytes 39337984 | tf_op jit(solution)/shard_map/sghij,sgjd->sighd/dot_general | solution.py:54
  61.2 1.3 copy.71
  62.6 10.1 %fusion.6 = bf16[8192,512]{0,1:T(8,128)(2,1)} fusion(bf16[512,8192]{1,0:T(8,128)(2,1)} %param.13, bf16[64,8,4,128]{3,2,1,0:T(4,128)(2,1)S(1)} %bitcast.123), kind=kOutput, calls=%fused_computation.8 | convolution fusion | flops 4299161600 | bytes 17301504 | tf_op jit(solution)/shard_map/dot_general | solution.py:103
  72.7 0.0 reduce-scatter.2.cloned.1.call-update
  72.7 109.6 %reduce-scatter.2.cloned.1.call-done = bf16[512,512]{0,1:T(8,128)(2,1)} async-done(((bf16[8192,512]{0,1:T(8,128)(2,1)}), bf16[512,512]{0,1:T(8,128)(2,1)}) %reduce-scatter.2.cloned.1.call-update) | async-done | bytes 524304 | tf_op jit(solution)/shard_map/reduce_scatter | solution.py:102
  182.3 1.3 multiply_reduce_fusion
  183.6 0.6 broadcast_in_dim.20
  184.2 5.8 %all-to-all-start = ((f32[16,1,512]{2,1,0:T(1,128)}), f32[16,1,512]{2,1,0:T(1,128)S(1)}, u32[]{:S(2)}, u32[]{:S(2)}) async-start(f32[16,1,512]{2,1,0:T(1,128)} %broadcast_in_dim.20), calls=%async_computation.1 | async-start | bytes 65536 | tf_op jit(solution)/shard_map/all_to_all | solution.py:23
  190.0 7.3 %all-to-all-done = f32[16,1,512]{2,1,0:T(1,128)S(1)} async-done(((f32[16,1,512]{2,1,0:T(1,128)}), f32[16,1,512]{2,1,0:T(1,128)S(1)}, u32[]{:S(2)}, u32[]{:S(2)}) %all-to-all-start) | async-done | bytes 32800 | tf_op jit(solution)/shard_map/all_to_all | solution.py:23
  197.4 2.0 multiply_convert_fusion
  (16 shorter events, 0.1 us)
Async XLA Ops:
  6.5 175.7 %reduce-scatter.2.cloned.1.call-start = ((), (), s32[]{:S(2)}) async-start(), calls=%async_computation.2 | async-start | bytes 8912896 | tf_op jit(solution)/shard_map/reduce_scatter | solution.py:102
  6.5 10.3 %collective-permute-start.1 = (bf16[4,2048,128]{2,1,0:T(8,128)(2,1)}, bf16[4,2048,128]{2,1,0:T(8,128)(2,1)}, u32[]{:S(2)}, u32[]{:S(2)}) collective-permute-start(bf16[4,2048,128]{2,1,0:T(8,128)(2,1)} %param.11), channel_id=1, source_target_pairs={{0,1},{1,0},{2,3},{3,2},{4,5},{5,4},{6,7},{7,6},{8,9},{9,8},{10,11... | collective-permute-start | bytes 6291464 | tf_op jit(solution)/shard_map/ppermute | solution.py:18
  9.7 6.7 %collective-permute-start.2 = (bf16[512,64]{0,1:T(8,128)(2,1)}, bf16[512,64]{0,1:T(8,128)(2,1)S(1)}, u32[]{:S(2)}, u32[]{:S(2)}) collective-permute-start(bf16[512,64]{0,1:T(8,128)(2,1)} %param.9), channel_id=1, source_target_pairs={{0,1},{1,0},{2,3},{3,2},{4,5},{5,4},{6,7},{7,6},{8,9},{9,8},{10,11... | collective-permute-start | bytes 196616 | tf_op jit(solution)/shard_map/ppermute | solution.py:18
  9.7 6.7 %collective-permute-start.3 = (bf16[512,64]{0,1:T(8,128)(2,1)}, bf16[512,64]{0,1:T(8,128)(2,1)S(1)}, u32[]{:S(2)}, u32[]{:S(2)}) collective-permute-start(bf16[512,64]{0,1:T(8,128)(2,1)} %param.10), channel_id=1, source_target_pairs={{0,1},{1,0},{2,3},{3,2},{4,5},{5,4},{6,7},{7,6},{8,9},{9,8},{10,11... | collective-permute-start | bytes 196616 | tf_op jit(solution)/shard_map/ppermute | solution.py:18
  13.2 33.1 %collective-permute-start = (bf16[4,2048,128]{1,2,0:T(8,128)(2,1)S(1)}, bf16[4,2048,128]{1,2,0:T(8,128)(2,1)}, u32[]{:S(2)}, u32[]{:S(2)}) collective-permute-start(bf16[4,2048,128]{1,2,0:T(8,128)(2,1)S(1)} %copy.57), channel_id=1, source_target_pairs={{0,1},{1,0},{2,3},{3,2},{4,5},{5,4},{6,7},{7,6},{8,9},{9,8},{10,11... | collective-permute-start | bytes 6291464 | tf_op jit(solution)/shard_map/ppermute | solution.py:18
  72.7 109.6 %copy-start = (bf16[512,512]{1,0:T(8,128)(2,1)S(1)}, bf16[512,512]{1,0:T(8,128)(2,1)}, u32[]{:S(2)}) copy-start(bf16[512,512]{1,0:T(8,128)(2,1)} %param.14) | copy-start | bytes 1572868
  72.7 117.3 %copy-start.1 = (bf16[512]{0:T(512)(128)(2,1)S(1)}, bf16[512]{0:T(512)(128)(2,1)}, u32[]{:S(2)}) copy-start(bf16[512]{0:T(512)(128)(2,1)} %param.15) | copy-start | bytes 3076
  184.2 13.1 %all-to-all-start = ((f32[16,1,512]{2,1,0:T(1,128)}), f32[16,1,512]{2,1,0:T(1,128)S(1)}, u32[]{:S(2)}, u32[]{:S(2)}) async-start(f32[16,1,512]{2,1,0:T(1,128)} %broadcast_in_dim.20), calls=%async_computation.1 | async-start | bytes 65536 | tf_op jit(solution)/shard_map/all_to_all | solution.py:23
Sparse Core Ops, SparseCore 0:
  72.8 109.3 reduce-scatter.1
where the time goes:
time: 207 us; the launch traced here: 206 us
  waiting for transfers between devices  117 us (57%)
  matrix products  41.1 us (20%)
  other arithmetic  17.2 us (8%)
  between operations  13.5 us (7%)
  starting transfers between devices  9.81 us (5%)
  local copies, waits for them, and re-layouts  7.81 us (4%)
    reduce_scatter x1, waiting for transfers between devices, per_device(): lax.psum_scatter(lax.dot_general(out_weight, attended, (((0,), (1,)), (()...  110 us
    dot_general x1, matrix products, attend_block(): jnp.einsum('sighd,sgjd->sghij', grouped, old_keys, preferred_element_type...  15.4 us
    dot_general x1, matrix products, attend_block(): jnp.einsum('sghij,sgjd->sighd', weights.astype(jnp.bfloat16), old_values,...  14.9 us
    reduce_sum x1, other arithmetic, attend_block(): total = jnp.sum(weights, axis=-1)  13.6 us
    dot_general x1, matrix products, per_device(): lax.dot_general(out_weight, attended, (((0,), (1,)), ((), ())), preferred...  10.1 us
    all_to_all x1, waiting for transfers between devices, sent_to_all(): return lax.all_to_all(copies, axis, split_axis=0, concat_axis=0, tiled=True)  7.29 us
    all_to_all x1, starting transfers between devices, sent_to_all(): return lax.all_to_all(copies, axis, split_axis=0, concat_axis=0, tiled=True)  5.82 us
  transfers between devices with their start and end apart: 6, of which 2 were waited for; matrix products, arithmetic and copies ran while one was open for 17% of the time, Pallas kernels for 0%

commit v1 on v0

v1 whole, which is shorter than its diff:
```python
import jax
import jax.numpy as jnp
from jax import lax
from jax.experimental import pallas as pl
from jax.experimental.pallas import tpu as pltpu
from jax.sharding import PartitionSpec as P

D = 8192
HD = 128
SPAN = 128
SEQS = 4
HALF = 2048
COLS = 512
EPSILON = 1e-05
SCALE = HD**-0.5 * 1.4426950408889634

MESH = pl.DeviceIdType.MESH
F32 = jnp.float32
BF16 = jnp.bfloat16

ORDER = ((2, 0), (2, 1), (1, 1), (3, 0), (1, 0), (3, 1), (0, 1), (0, 0))


def dot_t(a, b):
    return lax.dot_general(a, b, (((1,), (1,)), ((), ())), preferred_element_type=F32)


def dot(a, b):
    return jnp.dot(a, b, preferred_element_type=F32)


def with_ones(v):
    return jnp.concatenate([v, jnp.ones_like(v)], axis=1)


def kernel(
    q_hbm, nk_hbm, nv_hbm, ck_hbm, cv_hbm, w_hbm, res_hbm, gain_ref, out_ref,
    q_v, kown, vown, koth, voth, nk_own, nv_own, nk_oth, nv_oth, nk, nv,
    wown, woth, m_ref, acc_ref, aown, aoth, pbuf, fbuf, xbuf, r1, r2, rx,
    hid, res_v, ss, ssr,
    load_sem, kvl_sem, wl_sem,
    kv_send, kv_recv, nkv_send, nkv_recv, w_send, w_recv, a_send, a_recv,
    r1_send, r1_recv, r2_send, r2_recv, x_send, x_recv, ss_send, ss_recv,
):
    me = lax.axis_index("tp")
    core = lax.rem(me, 2)
    xh = lax.rem(lax.div(me, 2), 2)
    y = lax.div(me, 4)

    def peer(dy, dx, dc):
        py = lax.rem(y + dy, 4)
        px = lax.rem(xh + dx, 2)
        pc = lax.rem(core + dc, 2)
        return (py * 2 + px) * 2 + pc

    partner = peer(0, 0, 1)
    up, down, far, across = peer(1, 0, 0), peer(3, 0, 0), peer(2, 0, 0), peer(0, 1, 0)

    def remote(src, dst, send, recv, dev):
        return pltpu.make_async_remote_copy(
            src_ref=src, dst_ref=dst, send_sem=send, recv_sem=recv,
            device_id={"tp": dev}, device_id_type=MESH,
        )

    def kv_local(s):
        return (
            pltpu.make_async_copy(ck_hbm.at[s], kown.at[s], kvl_sem.at[s, 0]),
            pltpu.make_async_copy(cv_hbm.at[s], vown.at[s], kvl_sem.at[s, 1]),
        )

    def kv_remote(s):
        return (
            remote(ck_hbm.at[s], koth.at[s], kv_send.at[s, 0], kv_recv.at[s, 0], partner),
            remote(cv_hbm.at[s], voth.at[s], kv_send.at[s, 1], kv_recv.at[s, 1], partner),
        )

    def columns(slot, dc):
        dy, dx = ORDER[slot]
        start = peer(dy, dx, dc) * COLS
        return w_hbm.at[:, pl.ds(pl.multiple_of(start, COLS), COLS)]

    def w_local(slot):
        return pltpu.make_async_copy(columns(slot, 0), wown.at[slot], wl_sem.at[slot])

    def w_remote(slot):
        return remote(
            columns(slot, 1), woth.at[slot], w_send.at[slot], w_recv.at[slot], partner
        )

    def nkv_remote():
        return (
            remote(nk_hbm, nk_oth, nkv_send.at[0], nkv_recv.at[0], partner),
            remote(nv_hbm, nv_oth, nkv_send.at[1], nkv_recv.at[1], partner),
        )

    def attended_remote(s):
        return remote(aown.at[s], aoth.at[s], a_send.at[s], a_recv.at[s], partner)

    def first_remote(s):
        return (
            remote(pbuf.at[s, 0], r1.at[s, 0], r1_send.at[s, 0], r1_recv.at[s, 0], up),
            remote(pbuf.at[s, 1], r1.at[s, 1], r1_send.at[s, 1], r1_recv.at[s, 1], down),
        )

    def direct_remote(s):
        return (
            remote(pbuf.at[s, 2], r2.at[s, 1], r2_send.at[s, 1], r2_recv.at[s, 1], up),
            remote(pbuf.at[s, 3], r2.at[s, 2], r2_send.at[s, 2], r2_recv.at[s, 2], down),
        )

    def forward_remote(s):
        return (
            remote(fbuf.at[s, 0], r2.at[s, 0], r2_send.at[s, 0], r2_recv.at[s, 0], up),
            remote(fbuf.at[s, 1], r2.at[s, 3], r2_send.at[s, 3], r2_recv.at[s, 3], down),
        )

    def x_remote(s):
        return remote(xbuf.at[s], rx.at[s], x_send.at[s], x_recv.at[s], across)

    load = (
        pltpu.make_async_copy(q_hbm, q_v, load_sem.at[0]),
        pltpu.make_async_copy(nk_hbm, nk_own, load_sem.at[1]),
        pltpu.make_async_copy(nv_hbm, nv_own, load_sem.at[2]),
        pltpu.make_async_copy(res_hbm, res_v, load_sem.at[3]),
    )

    barrier = pltpu.get_barrier_semaphore()
    for dev in (partner, up, down, far, across):
        pl.semaphore_signal(barrier, inc=1, device_id={"tp": dev}, device_id_type=MESH)
    load[0].start()
    for copy in kv_local(0):
        copy.start()
    load[1].start()
    load[2].start()
    pl.semaphore_wait(barrier, 5)

    for copy in kv_remote(0) + nkv_remote():
        copy.start()
    for slot in range(4):
        w_remote(slot).start()
    for s in range(1, SEQS):
        for copy in kv_local(s):
            copy.start()
    for slot in range(8):
        w_local(slot).start()
    load[3].start()

    def rows_of(s):
        part = q_v[pl.ds(pl.multiple_of(s * SPAN, SPAN), SPAN), :]
        return jnp.concatenate([part[:, h * HD : (h + 1) * HD] for h in range(4)], axis=0)

    def own_half(s):
        for copy in kv_local(s):
            copy.wait()
        scores = dot_t(rows_of(s), kown[s])
        peak = jnp.max(scores, axis=1, keepdims=True)
        weights = jnp.exp2((scores - peak) * SCALE).astype(BF16)
        acc_ref[...] = dot(weights, with_ones(vown[s]))
        m_ref[...] = jnp.broadcast_to(peak, m_ref.shape)

    def other_half(s):
        for copy in kv_remote(s):
            copy.wait_recv()
        q = rows_of(s)
        tokens = pl.ds(pl.multiple_of(s * SPAN, SPAN), SPAN)
        scores = dot_t(q, koth[s])
        recent = dot_t(q, nk[tokens, :])
        row = lax.rem(lax.broadcasted_iota(jnp.int32, recent.shape, 0), SPAN)
        col = lax.broadcasted_iota(jnp.int32, recent.shape, 1)
        recent = jnp.where(row >= col, recent, -jnp.inf)
        old = m_ref[:, :1]
        peak = jnp.maximum(
            jnp.max(scores, axis=1, keepdims=True), jnp.max(recent, axis=1, keepdims=True)
        )
        peak = jnp.maximum(peak, old)
        weights = jnp.exp2((scores - peak) * SCALE).astype(BF16)
        recent_weights = jnp.exp2((recent - peak) * SCALE).astype(BF16)
        mixed = acc_ref[...] * jnp.exp2((old - peak) * SCALE)
        mixed = mixed + dot(weights, with_ones(voth[s]))
        mixed = mixed + dot(recent_weights, with_ones(nv[tokens, :]))
        result = (mixed[:, :HD] / mixed[:, HD:]).astype(BF16)
        for h in range(4):
            aown[s, :, h * HD : (h + 1) * HD] = result[h * SPAN : (h + 1) * SPAN, :]

    def project(s):
        attended_remote(s).wait_recv()
        for slot in range(8):
            block = dot(aown[s], wown[slot]) + dot(aoth[s], woth[slot])
            pbuf[s, slot] = block.astype(BF16)
            if slot < 2:
                first_remote(s)[slot].start()
            elif slot < 4:
                direct_remote(s)[slot - 2].start()

    def forward(s):
        for i, copy in enumerate(first_remote(s)):
            copy.wait_recv()
            fbuf[s, i] = (r1[s, i].astype(F32) + pbuf[s, 4 + i].astype(F32)).astype(BF16)
            forward_remote(s)[i].start()

    def send_across(s):
        direct_remote(s)[0].wait_recv()
        forward_remote(s)[1].wait_recv()
        total = pbuf[s, 6].astype(F32) + r2[s, 1].astype(F32) + r2[s, 3].astype(F32)
        xbuf[s] = total.astype(BF16)
        x_remote(s).start()

    def to_row(column):
        return jnp.transpose(jnp.broadcast_to(column, (SPAN, SPAN)))[:8, :]

    def finish(s):
        direct_remote(s)[1].wait_recv()
        forward_remote(s)[0].wait_recv()
        x_remote(s).wait_recv()
        tokens = pl.ds(pl.multiple_of(s * SPAN, SPAN), SPAN)
        total = pbuf[s, 7].astype(F32) + r2[s, 0].astype(F32) + r2[s, 2].astype(F32)
        total = total + rx[s].astype(F32) + res_v[tokens, :].astype(F32)
        hid[s] = total
        ss[0, s] = to_row(jnp.sum(total * total, axis=1, keepdims=True))

    load[0].wait()
    own_half(0)

    for copy in load[1:3]:
        copy.wait()
    for copy in nkv_remote():
        copy.wait_recv()
    lane = lax.broadcasted_iota(jnp.int32, (64, HD), 1)
    line = lax.broadcasted_iota(jnp.int32, (64, HD), 0)
    mine = (lane == line + 64 * core).astype(F32).astype(BF16)
    theirs = (lane == line + 64 * (1 - core)).astype(F32).astype(BF16)
    nk[...] = (dot(nk_own[...], mine) + dot(nk_oth[...], theirs)).astype(BF16)
    nv[...] = (dot(nv_own[...], mine) + dot(nv_oth[...], theirs)).astype(BF16)
    for slot in range(8):
        w_local(slot).wait()
    load[3].wait()

    def sequence(s, carry):
        other_half(s)
        attended_remote(s).start()

        @pl.when(s == 0)
        def _():
            for slot in range(4, 8):
                w_remote(slot).start()

        @pl.when(s < SEQS - 1)
        def _():
            for copy in kv_remote(s + 1):
                copy.start()
            own_half(s + 1)

        @pl.when(s >= 1)
        def _():
            forward(s - 1)

        @pl.when(s >= 2)
        def _():
            send_across(s - 2)

        @pl.when(s == 0)
        def _():
            for slot in range(8):
                w_remote(slot).wait_recv()

        project(s)
        return carry

    lax.fori_loop(0, SEQS, sequence, 0)

    forward(SEQS - 1)
    send_across(SEQS - 2)
    finish(0)
    finish(1)
    send_across(SEQS - 1)
    finish(2)
    finish(3)

    def exchange(i, source, dev):
        return remote(ss.at[source], ssr.at[i], ss_send.at[i], ss_recv.at[i], dev)

    copies = [exchange(0, 0, partner)]
    copies[0].start()
    copies[0].wait_recv()
    ss[1] = ss[0] + ssr[0]
    copies.append(exchange(1, 1, across))
    copies[1].start()
    copies[1].wait_recv()
    ss[2] = ss[1] + ssr[1]
    for i, dev in enumerate((up, down, far)):
        copies.append(exchange(2 + i, 2, dev))
        copies[-1].start()
    for copy in copies[2:]:
        copy.wait_recv()
    ss[3] = ss[2] + ssr[2] + ssr[3] + ssr[4]

    for s in range(SEQS):
        row = lax.rsqrt(ss[3, s] * (1.0 / D) + EPSILON)[:1, :]
        column = jnp.transpose(jnp.broadcast_to(row, (SPAN, SPAN)))[:, :1]
        out_ref[s * SPAN : (s + 1) * SPAN, :] = (hid[s] * column * gain_ref[...]).astype(BF16)

    for copy in copies:
        copy.wait_send()
    for copy in nkv_remote():
        copy.wait_send()
    for slot in range(8):
        w_remote(slot).wait_send()

    def drain(s, carry):
        for copy in kv_remote(s) + first_remote(s) + direct_remote(s) + forward_remote(s):
            copy.wait_send()
        attended_remote(s).wait_send()
        x_remote(s).wait_send()
        return carry

    lax.fori_loop(0, SEQS, drain, 0)


def per_device(queries, new_keys, new_values, cache_keys, cache_values, out_weight, residual, gain):
    any_spec = pl.BlockSpec(memory_space=pl.ANY)
    vmem_spec = pl.BlockSpec(memory_space=pltpu.VMEM)
    dma = pltpu.SemaphoreType.DMA
    block = (SPAN, COLS)
    return pl.pallas_call(
        kernel,
        name="attend",
        out_shape=jax.ShapeDtypeStruct((SEQS * SPAN, COLS), BF16),
        in_specs=[any_spec] * 7 + [vmem_spec],
        out_specs=vmem_spec,
        scratch_shapes=[
            pltpu.VMEM((SEQS * SPAN, 4 * HD), BF16),
            *[pltpu.VMEM((SEQS, HALF, HD), BF16)] * 4,
            *[pltpu.VMEM((SEQS * SPAN, HD // 2), BF16)] * 4,
            *[pltpu.VMEM((SEQS * SPAN, HD), BF16)] * 2,
            *[pltpu.VMEM((8, COLS, COLS), BF16)] * 2,
            pltpu.VMEM((4 * SPAN, HD), F32),
            pltpu.VMEM((4 * SPAN, 2 * HD), F32),
            *[pltpu.VMEM((SEQS, *block), BF16)] * 2,
            pltpu.VMEM((SEQS, 8, *block), BF16),
            pltpu.VMEM((SEQS, 2, *block), BF16),
            pltpu.VMEM((SEQS, *block), BF16),
            pltpu.VMEM((SEQS, 2, *block), BF16),
            pltpu.VMEM((SEQS, 4, *block), BF16),
            pltpu.VMEM((SEQS, *block), BF16),
            pltpu.VMEM((SEQS, *block), F32),
            pltpu.VMEM((SEQS * SPAN, COLS), BF16),
            pltpu.VMEM((4, SEQS, 8, SPAN), F32),
            pltpu.VMEM((5, SEQS, 8, SPAN), F32),
            dma((4,)), dma((SEQS, 2)), dma((8,)),
            dma((SEQS, 2)), dma((SEQS, 2)), dma((2,)), dma((2,)),
            dma((8,)), dma((8,)), dma((SEQS,)), dma((SEQS,)),
            dma((SEQS, 2)), dma((SEQS, 2)), dma((SEQS, 4)), dma((SEQS, 4)),
            dma((SEQS,)), dma((SEQS,)), dma((5,)), dma((5,)),
        ],
        compiler_params=pltpu.CompilerParams(
            collective_id=0, has_side_effects=True, vmem_limit_bytes=60 * 2**20
        ),
    )(
        queries, new_keys, new_values, cache_keys, cache_values, out_weight, residual,
        gain.astype(F32)[None, :],
    )


def solution(mesh):
    in_specs = (
        P("dp", "tp"),
        P("dp", "tp"),
        P("dp", "tp"),
        P("dp", "tp", None),
        P("dp", "tp", None),
        P("tp", None),
        P("dp", "tp"),
        P("tp"),
    )
    return jax.shard_map(
        per_device, mesh=mesh, in_specs=in_specs, out_specs=P("dp", "tp"), check_vma=False
    )
```

time: 207 us -> 74.5 us (0.36)
  waiting for transfers between devices: 117 us -> 0 us
  Pallas kernels: 0 us -> 68 us
  matrix products: 41.1 us -> 0 us
  other arithmetic: 17.2 us -> 1.22 us
  between operations: 13.5 us -> 0.01 us
  starting transfers between devices: 9.81 us -> 0 us
  local copies, waits for them, and re-layouts: 7.81 us -> 5.06 us
    reduce_scatter x1 -> x0, waiting for transfers between devices: 110 us -> none  [per_device(): lax.psum_scatter(lax.dot_general(out_weight, attended, (((0,), (1,)), (()...]
    pallas_call x0 -> x1, Pallas kernels: none -> 68 us  [per_device(): pl.pallas_call(kernel, name='attend', out_shape=jax.ShapeDtypeStruct((SEQ...]
    dot_general x5 -> x0, matrix products: 41.1 us -> none  [the longest x1 15.4 us: attend_block(): jnp.einsum('sighd,sgjd->sghij', grouped, old_keys, preferred_element_type...]
    reduce_sum x4 -> x0, other arithmetic: 15.1 us -> none  [the longest x1 13.6 us: attend_block(): total = jnp.sum(weights, axis=-1)]
    all_to_all x1 -> x0, waiting for transfers between devices: 7.29 us -> none  [sent_to_all(): return lax.all_to_all(copies, axis, split_axis=0, concat_axis=0, tiled=True)]
    all_to_all x1 -> x0, starting transfers between devices: 5.82 us -> none  [sent_to_all(): return lax.all_to_all(copies, axis, split_axis=0, concat_axis=0, tiled=True)]
    ppermute x4 -> x0, starting transfers between devices: 3.98 us -> none  [partner(): return lax.ppermute(value, axis, pairs)]
    unnamed x5 -> x3, local copies, waits for them, and re-layouts: 2.94 us -> 5.06 us
  transfers between devices with their start and end apart: 6 -> 0, of which waited for: 2 -> 0; matrix products, arithmetic and copies ran while one was open for 17% -> 0% of each run, Pallas kernels for 0% -> 0%
where the time goes in v1:
time: 74.5 us; the launch traced here: 74.2 us
  Pallas kernels  68 us (91%)
  local copies, waits for them, and re-layouts  5.06 us (7%)
  other arithmetic  1.22 us (2%)
    pallas_call x1, Pallas kernels, per_device(): pl.pallas_call(kernel, name='attend', out_shape=jax.ShapeDtypeStruct((SEQ...  68 us
    unnamed x3, local copies, waits for them, and re-layouts  5.06 us

profile of v1, /device:TPU:1, one launch (start us, length us, event | category | flops | bytes accessed | tf_op | source)
XLA Modules:
  0.0 74.2 jit_solution(15611076513733630426)
XLA Ops:
  0.0 1.2 %broadcast_in_dim.7 = f32[512]{0:T(512)} convert(bf16[512]{0:T(512)(128)(2,1)} %param.15) | non-fusion elementwise | flops 512 | bytes 3072 | tf_op jit(solution)/shard_map/broadcast_in_dim | solution.py:360
  1.2 1.6 %copy.9.nk_hbm = bf16[512,64]{1,0:T(8,128)(2,1)} copy(bf16[512,64]{0,1:T(8,128)(2,1)} %param.9) | data formatting | bytes 131072 | tf_op args[1]
  2.8 1.6 %copy.10.nv_hbm = bf16[512,64]{1,0:T(8,128)(2,1)} copy(bf16[512,64]{0,1:T(8,128)(2,1)} %param.10) | data formatting | bytes 131072 | tf_op args[2]
  4.4 68.0 %attend.1 = bf16[512,512]{1,0:T(8,128)(2,1)} custom-call(bf16[512,512]{1,0:T(8,128)(2,1)} %q_hbm.1, bf16[512,64]{1,0:T(8,128)(2,1)} %copy.9.nk_hbm, bf16[512,64]{1,0:T(8,128)(2,1)} %copy.10.nv_hbm, bf16[4,2048,128]{2,1,0:T(8,128)(2,1)} %ck_hbm.1, bf16[4,2048,128]{2,1,0:T(8,128)(2,1)} %cv_hbm.1, bf16[512,8192]{1,0:T(8,128)(2,1)} %w_hbm.1, ...), custom_call_target="tpu_custom_call" | custom-call | tf_op jit(solution)/shard_map/attend/pallas_call | solution.py:324
  72.4 1.9 %copy.12 = bf16[512,512]{1,0:T(8,128)(2,1)} copy(bf16[512,512]{1,0:T(8,128)(2,1)} %attend.1) | data formatting | bytes 1048576

commit v2 on v1

v2 whole, which is shorter than its diff:
```python
import jax
import jax.numpy as jnp
from jax import lax
from jax.experimental import pallas as pl
from jax.experimental.pallas import tpu as pltpu
from jax.sharding import PartitionSpec as P

D = 8192
HD = 128
SPAN = 128
SEQS = 4
HALF = 2048
COLS = 512
EPSILON = 1e-05
SCALE = HD**-0.5 * 1.4426950408889634

MESH = pl.DeviceIdType.MESH
F32 = jnp.float32
BF16 = jnp.bfloat16

ORDER = ((2, 1), (2, 0), (1, 1), (3, 0), (3, 1), (0, 1), (1, 0), (0, 0))
SLOT = {key: slot for slot, key in enumerate(ORDER)}
WIDE = COLS // 2
HEADS = 2
ROWS = HEADS * SPAN
CHUNKS = 4 // HEADS
TALL = SPAN // 2


def dot_t(a, b):
    return lax.dot_general(a, b, (((1,), (1,)), ((), ())), preferred_element_type=F32)


def dot(a, b):
    return jnp.dot(a, b, preferred_element_type=F32)


def with_ones(v, axis=1):
    return jnp.concatenate([v, jnp.ones_like(v)], axis=axis)


def kernel(
    q_hbm, nk_hbm, nv_hbm, ck_hbm, cv_hbm, w_hbm, res_hbm, gain_ref, out_ref,
    q_v, kown, vown, koth, voth, nk, nv, wown, woth, m_ref, acc_ref, aown, aoth,
    pbuf, fbuf, xbuf, r1, r2, rx, rxx, cbuf, gbuf, q1, q2, hid, res_v, ss, ssr,
    load_sem, kvl_sem, wl_sem,
    kv_send, kv_recv, nkv_send, nkv_recv, w_send, w_recv, a_send, a_recv,
    r1_send, r1_recv, r2_send, r2_recv, x_send, x_recv, xx_send, xx_recv,
    q1_send, q1_recv, q2_send, q2_recv, ss_send, ss_recv,
):
    me = lax.axis_index("tp")
    core = lax.rem(me, 2)
    xh = lax.rem(lax.div(me, 2), 2)
    y = lax.div(me, 4)
    half = pl.ds(pl.multiple_of(core * (HD // 2), HD // 2), HD // 2)

    def peer(dy, dx, dc):
        py = lax.rem(y + dy, 4)
        px = lax.rem(xh + dx, 2)
        pc = lax.rem(core + dc, 2)
        return (py * 2 + px) * 2 + pc

    partner = peer(0, 0, 1)
    up, down, far, across = peer(1, 0, 0), peer(3, 0, 0), peer(2, 0, 0), peer(0, 1, 0)

    def remote(src, dst, send, recv, dev):
        return pltpu.make_async_remote_copy(
            src_ref=src, dst_ref=dst, send_sem=send, recv_sem=recv,
            device_id={"tp": dev}, device_id_type=MESH,
        )

    def kv_local(s):
        return (
            pltpu.make_async_copy(ck_hbm.at[s], kown.at[s], kvl_sem.at[s, 0]),
            pltpu.make_async_copy(cv_hbm.at[s], vown.at[s], kvl_sem.at[s, 1]),
        )

    def kv_remote(s):
        return (
            remote(ck_hbm.at[s], koth.at[s], kv_send.at[s, 0], kv_recv.at[s, 0], partner),
            remote(cv_hbm.at[s], voth.at[s], kv_send.at[s, 1], kv_recv.at[s, 1], partner),
        )

    def columns(slot, dc):
        dy, dx = ORDER[slot]
        start = peer(dy, dx, dc) * COLS
        return w_hbm.at[:, pl.ds(pl.multiple_of(start, COLS), COLS)]

    def w_local(slot):
        return pltpu.make_async_copy(columns(slot, 0), wown.at[slot], wl_sem.at[slot])

    def w_remote(slot):
        return remote(
            columns(slot, 1), woth.at[slot], w_send.at[slot], w_recv.at[slot], partner
        )

    def nkv_remote():
        return (
            remote(nk_hbm, nk.at[half], nkv_send.at[0], nkv_recv.at[0], partner),
            remote(nv_hbm, nv.at[half], nkv_send.at[1], nkv_recv.at[1], partner),
        )

    def attended_remote(s):
        return remote(aown.at[s], aoth.at[s], a_send.at[s], a_recv.at[s], partner)

    def first_remote(s):
        return (
            remote(pbuf.at[s, SLOT[2, 0], 0], r1.at[s, 0], r1_send.at[s, 0], r1_recv.at[s, 0], up),
            remote(pbuf.at[s, SLOT[2, 1], 0], r1.at[s, 1], r1_send.at[s, 1], r1_recv.at[s, 1], down),
        )

    def direct_remote(s):
        return (
            remote(pbuf.at[s, SLOT[1, 1], 0], r2.at[s, 1], r2_send.at[s, 1], r2_recv.at[s, 1], up),
            remote(pbuf.at[s, SLOT[3, 0], 0], r2.at[s, 2], r2_send.at[s, 2], r2_recv.at[s, 2], down),
        )

    def forward_remote(s):
        return (
            remote(fbuf.at[s, 0], r2.at[s, 0], r2_send.at[s, 0], r2_recv.at[s, 0], up),
            remote(fbuf.at[s, 1], r2.at[s, 3], r2_send.at[s, 3], r2_recv.at[s, 3], down),
        )

    def x_remote(s):
        return remote(xbuf.at[s], rx.at[s], x_send.at[s], x_recv.at[s], across)

    def x_first_remote(s, dy):
        return remote(
            pbuf.at[s, SLOT[dy, 1], 1], rxx.at[s, dy], xx_send.at[s, dy], xx_recv.at[s, dy], across
        )

    def low_high(ref, s, i, high):
        return ref.at[s, i, pl.ds(high * TALL, TALL)]

    def y_first_remote(s):
        return (
            remote(low_high(cbuf, s, 0, 0), q1.at[s, 0], q1_send.at[s, 0], q1_recv.at[s, 0], up),
            remote(low_high(cbuf, s, 0, 1), q1.at[s, 1], q1_send.at[s, 1], q1_recv.at[s, 1], down),
        )

    def y_direct_remote(s):
        return (
            remote(
                low_high(cbuf, s, 1, 1), low_high(q2, s, 0, 1),
                q2_send.at[s, 1], q2_recv.at[s, 1], up,
            ),
            remote(
                low_high(cbuf, s, 2, 0), low_high(q2, s, 1, 0),
                q2_send.at[s, 2], q2_recv.at[s, 2], down,
            ),
        )

    def y_forward_remote(s):
        return (
            remote(gbuf.at[s, 0], low_high(q2, s, 0, 0), q2_send.at[s, 0], q2_recv.at[s, 0], up),
            remote(gbuf.at[s, 1], low_high(q2, s, 1, 1), q2_send.at[s, 3], q2_recv.at[s, 3], down),
        )

    others = [(dy, dx, dc) for dy in range(4) for dx in range(2) for dc in range(2)][1:]

    def square_remote(i):
        return remote(ss, ssr.at[i], ss_send.at[i], ss_recv.at[i], peer(*others[i]))

    load = (
        pltpu.make_async_copy(q_hbm, q_v, load_sem.at[0]),
        pltpu.make_async_copy(nk_hbm, nk.at[half], load_sem.at[1]),
        pltpu.make_async_copy(nv_hbm, nv.at[half], load_sem.at[2]),
        pltpu.make_async_copy(res_hbm, res_v, load_sem.at[3]),
    )

    barrier = pltpu.get_barrier_semaphore()
    for dev in (partner, up, down, far, across):
        pl.semaphore_signal(barrier, inc=1, device_id={"tp": dev}, device_id_type=MESH)
    load[0].start()
    for copy in kv_local(0):
        copy.start()
    load[1].start()
    load[2].start()
    pl.semaphore_wait(barrier, 5)

    for copy in kv_remote(0) + nkv_remote():
        copy.start()
    for slot in range(4):
        w_remote(slot).start()
    for s in range(1, SEQS):
        for copy in kv_local(s):
            copy.start()
    for slot in range(8):
        w_local(slot).start()
    load[3].start()

    def rows_of(s, chunk):
        part = q_v[pl.ds(pl.multiple_of(s * SPAN, SPAN), SPAN), :]
        heads = range(chunk * HEADS, (chunk + 1) * HEADS)
        return jnp.concatenate([part[:, h * HD : (h + 1) * HD] for h in heads], axis=0)

    def chunk_rows(chunk):
        return slice(chunk * ROWS, (chunk + 1) * ROWS)

    def own_half(s):
        for copy in kv_local(s):
            copy.wait()
        upcoming = dot_t(rows_of(s, 0), kown[s])
        for chunk in range(CHUNKS):
            scores = upcoming
            if chunk + 1 < CHUNKS:
                upcoming = dot_t(rows_of(s, chunk + 1), kown[s])
            rows = chunk_rows(chunk)
            peak = jnp.max(scores, axis=1, keepdims=True)
            weights = jnp.exp2((scores - peak) * SCALE).astype(BF16)
            acc_ref[rows, :] = dot(weights, with_ones(vown[s]))
            m_ref[rows, :] = jnp.broadcast_to(peak, (ROWS, HD))

    def other_half(s):
        for copy in kv_remote(s):
            copy.wait_recv()
        tokens = pl.ds(pl.multiple_of(s * SPAN, SPAN), SPAN)

        def scores_of(chunk):
            q = rows_of(s, chunk)
            recent = dot(q, nk[:, tokens])
            row = lax.rem(lax.broadcasted_iota(jnp.int32, recent.shape, 0), SPAN)
            col = lax.broadcasted_iota(jnp.int32, recent.shape, 1)
            return dot_t(q, koth[s]), jnp.where(row >= col, recent, -jnp.inf)

        upcoming = scores_of(0)
        for chunk in range(CHUNKS):
            scores, recent = upcoming
            if chunk + 1 < CHUNKS:
                upcoming = scores_of(chunk + 1)
            rows = chunk_rows(chunk)
            old = m_ref[rows, :1]
            peak = jnp.maximum(
                jnp.max(scores, axis=1, keepdims=True), jnp.max(recent, axis=1, keepdims=True)
            )
            peak = jnp.maximum(peak, old)
            weights = jnp.exp2((scores - peak) * SCALE).astype(BF16)
            recent_weights = jnp.exp2((recent - peak) * SCALE).astype(BF16)
            mixed = acc_ref[rows, :] * jnp.exp2((old - peak) * SCALE)
            mixed = mixed + dot(weights, with_ones(voth[s]))
            mixed = mixed + dot_t(recent_weights, with_ones(nv[:, tokens], 0))
            result = (mixed[:, :HD] / mixed[:, HD:]).astype(BF16)
            for i in range(HEADS):
                h = chunk * HEADS + i
                aown[s, :, h * HD : (h + 1) * HD] = result[i * SPAN : (i + 1) * SPAN, :]

    def project(s):
        attended_remote(s).wait_recv()
        for slot, (dy, dx) in enumerate(ORDER):
            @pl.when(s == 0)
            def _():
                w_local(slot).wait()
                w_remote(slot).wait_recv()

            block = (dot(aown[s], wown[slot]) + dot(aoth[s], woth[slot])).astype(BF16)
            pbuf[s, slot, 0] = block[:, :WIDE]
            pbuf[s, slot, 1] = block[:, WIDE:]
            if dx == 1:
                x_first_remote(s, dy).start()
            if dy == 2:
                first_remote(s)[dx].start()
            elif (dy, dx) == (1, 1):
                direct_remote(s)[0].start()
            elif (dy, dx) == (3, 0):
                direct_remote(s)[1].start()

    def wide(ref):
        return ref.astype(F32)

    def forward(s):
        for i, slot in enumerate((SLOT[1, 0], SLOT[3, 1])):
            first_remote(s)[i].wait_recv()
            fbuf[s, i] = (wide(r1[s, i]) + wide(pbuf[s, slot, 0])).astype(BF16)
            forward_remote(s)[i].start()

    def send_across(s):
        direct_remote(s)[0].wait_recv()
        forward_remote(s)[1].wait_recv()
        total = wide(pbuf[s, SLOT[0, 1], 0]) + wide(r2[s, 1]) + wide(r2[s, 3])
        xbuf[s] = total.astype(BF16)
        x_remote(s).start()

    def sum_across(s):
        for i, dy in enumerate((2, 1, 3)):
            x_first_remote(s, dy).wait_recv()
            cbuf[s, i] = (wide(pbuf[s, SLOT[dy, 0], 1]) + wide(rxx[s, dy])).astype(BF16)
            if i == 0:
                for copy in y_first_remote(s):
                    copy.start()
            else:
                y_direct_remote(s)[i - 1].start()

    def y_forward(s):
        for i in range(2):
            y_first_remote(s)[i].wait_recv()
            kept = cbuf[s, 1 + i, i * TALL : (i + 1) * TALL, :]
            gbuf[s, i] = (wide(q1[s, i]) + wide(kept)).astype(BF16)
            y_forward_remote(s)[i].start()

    def finish(s):
        tokens = pl.ds(pl.multiple_of(s * SPAN, SPAN), SPAN)
        direct_remote(s)[1].wait_recv()
        forward_remote(s)[0].wait_recv()
        x_remote(s).wait_recv()
        left = wide(pbuf[s, SLOT[0, 0], 0]) + wide(r2[s, 0]) + wide(r2[s, 2]) + wide(rx[s])
        left = left + wide(res_v[tokens, :WIDE])
        hid[s, :, :WIDE] = left
        x_first_remote(s, 0).wait_recv()
        for copy in y_direct_remote(s) + y_forward_remote(s):
            copy.wait_recv()
        right = wide(pbuf[s, SLOT[0, 0], 1]) + wide(rxx[s, 0]) + wide(q2[s, 0]) + wide(q2[s, 1])
        right = right + wide(res_v[tokens, WIDE:])
        hid[s, :, WIDE:] = right
        column = jnp.sum(left * left + right * right, axis=1, keepdims=True)
        ss[s : s + 1, :] = jnp.transpose(jnp.broadcast_to(column, (SPAN, SPAN)))[:1, :]

    load[0].wait()

    def sequence(s, carry):
        own_half(s)

        @pl.when(s >= 1)
        def _():
            forward(s - 1)

        @pl.when(s >= 2)
        def _():
            y_forward(s - 2)
            send_across(s - 2)

        @pl.when(s == 0)
        def _():
            for copy in load[1:3]:
                copy.wait()
            for copy in nkv_remote():
                copy.wait_recv()

        other_half(s)
        attended_remote(s).start()

        @pl.when(s == 0)
        def _():
            for slot in range(4, 8):
                w_remote(slot).start()

        @pl.when(s < SEQS - 1)
        def _():
            for copy in kv_remote(s + 1):
                copy.start()

        @pl.when(s >= 1)
        def _():
            sum_across(s - 1)

        project(s)
        return carry

    lax.fori_loop(0, SEQS, sequence, 0)

    load[3].wait()
    ss[...] = jnp.zeros_like(ss)
    y_forward(SEQS - 2)
    send_across(SEQS - 2)
    finish(0)
    finish(1)
    forward(SEQS - 1)
    sum_across(SEQS - 1)
    finish(2)
    send_across(SEQS - 1)
    y_forward(SEQS - 1)
    finish(3)

    for i in range(15):
        square_remote(i).start()

    for copy in nkv_remote():
        copy.wait_send()
    for slot in range(8):
        w_remote(slot).wait_send()

    def drain(s, carry):
        for copy in kv_remote(s) + first_remote(s) + direct_remote(s) + forward_remote(s):
            copy.wait_send()
        for copy in y_first_remote(s) + y_direct_remote(s) + y_forward_remote(s):
            copy.wait_send()
        for dy in range(4):
            x_first_remote(s, dy).wait_send()
        attended_remote(s).wait_send()
        x_remote(s).wait_send()
        return carry

    lax.fori_loop(0, SEQS, drain, 0)

    lines = gain_ref[...].astype(F32)
    gain = jnp.concatenate([lines[i : i + 1, :] for i in range(4)], axis=1)
    for i in range(15):
        square_remote(i).wait_recv()
    squares = ss[...]
    for i in range(15):
        squares = squares + ssr[i]
    rows = lax.rsqrt(squares * (1.0 / D) + EPSILON)
    for s in range(SEQS):
        column = jnp.transpose(jnp.broadcast_to(rows[s : s + 1, :], (SPAN, SPAN)))[:, :1]
        out_ref[s * SPAN : (s + 1) * SPAN, :] = (hid[s] * column * gain).astype(BF16)
    for i in range(15):
        square_remote(i).wait_send()


def per_device(queries, new_keys, new_values, cache_keys, cache_values, out_weight, residual, gain):
    any_spec = pl.BlockSpec(memory_space=pl.ANY)
    vmem_spec = pl.BlockSpec(memory_space=pltpu.VMEM)
    dma = pltpu.SemaphoreType.DMA
    block = (SPAN, WIDE)
    return pl.pallas_call(
        kernel,
        name="attend",
        out_shape=pltpu.VMEM((SEQS * SPAN, COLS), BF16),
        in_specs=[any_spec] * 7 + [vmem_spec],
        out_specs=vmem_spec,
        scratch_shapes=[
            pltpu.VMEM((SEQS * SPAN, 4 * HD), BF16),
            *[pltpu.VMEM((SEQS, HALF, HD), BF16)] * 4,
            *[pltpu.VMEM((HD, SEQS * SPAN), BF16)] * 2,
            *[pltpu.VMEM((8, COLS, COLS), BF16)] * 2,
            pltpu.VMEM((4 * SPAN, HD), F32),
            pltpu.VMEM((4 * SPAN, 2 * HD), F32),
            *[pltpu.VMEM((SEQS, SPAN, COLS), BF16)] * 2,
            pltpu.VMEM((SEQS, 8, 2, *block), BF16),
            pltpu.VMEM((SEQS, 2, *block), BF16),
            pltpu.VMEM((SEQS, *block), BF16),
            pltpu.VMEM((SEQS, 2, *block), BF16),
            pltpu.VMEM((SEQS, 4, *block), BF16),
            pltpu.VMEM((SEQS, *block), BF16),
            pltpu.VMEM((SEQS, 4, *block), BF16),
            pltpu.VMEM((SEQS, 3, *block), BF16),
            pltpu.VMEM((SEQS, 2, TALL, WIDE), BF16),
            pltpu.VMEM((SEQS, 2, TALL, WIDE), BF16),
            pltpu.VMEM((SEQS, 2, *block), BF16),
            pltpu.VMEM((SEQS, SPAN, COLS), F32),
            pltpu.VMEM((SEQS * SPAN, COLS), BF16),
            pltpu.VMEM((8, SPAN), F32),
            pltpu.VMEM((15, 8, SPAN), F32),
            dma((4,)), dma((SEQS, 2)), dma((8,)),
            dma((SEQS, 2)), dma((SEQS, 2)), dma((2,)), dma((2,)),
            dma((8,)), dma((8,)), dma((SEQS,)), dma((SEQS,)),
            dma((SEQS, 2)), dma((SEQS, 2)), dma((SEQS, 4)), dma((SEQS, 4)),
            dma((SEQS,)), dma((SEQS,)), dma((SEQS, 4)), dma((SEQS, 4)),
            dma((SEQS, 2)), dma((SEQS, 2)), dma((SEQS, 4)), dma((SEQS, 4)),
            dma((15,)), dma((15,)),
        ],
        compiler_params=pltpu.CompilerParams(
            collective_id=0, has_side_effects=True, vmem_limit_bytes=60 * 2**20
        ),
    )(
        queries, new_keys.T, new_values.T, cache_keys, cache_values, out_weight, residual,
        gain.reshape(4, 128),
    )


def solution(mesh):
    in_specs = (
        P("dp", "tp"),
        P("dp", "tp"),
        P("dp", "tp"),
        P("dp", "tp", None),
        P("dp", "tp", None),
        P("tp", None),
        P("dp", "tp"),
        P("tp"),
    )
    return jax.shard_map(
        per_device, mesh=mesh, in_specs=in_specs, out_specs=P("dp", "tp"), check_vma=False
    )
```

time: 74.5 us -> 58 us (0.78)
  Pallas kernels: 68 us -> 57.1 us
  local copies, waits for them, and re-layouts: 5.06 us -> 0.8 us
  other arithmetic: 1.22 us -> 0 us
    pallas_call x1, Pallas kernels: 68 us -> 57.1 us  [per_device(): pl.pallas_call(kernel, name='attend', out_shape=pltpu.VMEM((SEQS * SPAN,...]
    unnamed x3 -> x1, local copies, waits for them, and re-layouts: 5.06 us -> 0.8 us
    broadcast_in_dim x1 -> x0, other arithmetic: 1.22 us -> none  [per_device(): gain.astype(F32)[None, :]]
where the time goes in v2:
time: 58 us; the launch traced here: 57.9 us
  Pallas kernels  57.1 us (98%)
  local copies, waits for them, and re-layouts  0.8 us (1%)
    pallas_call x1, Pallas kernels, per_device(): pl.pallas_call(kernel, name='attend', out_shape=pltpu.VMEM((SEQS * SPAN,...  57.1 us

profile of v2, /device:TPU:1, one launch (start us, length us, event | category | flops | bytes accessed | tf_op | source)
XLA Modules:
  0.0 57.9 jit_solution(9442985697394738239)
XLA Ops:
  0.0 57.1 %attend.1 = bf16[512,512]{1,0:T(8,128)(2,1)S(1)} custom-call(bf16[512,512]{1,0:T(8,128)(2,1)} %q_hbm.1, bf16[64,512]{1,0:T(8,128)(2,1)} %bitcast.3, bf16[64,512]{1,0:T(8,128)(2,1)} %bitcast.4, bf16[4,2048,128]{2,1,0:T(8,128)(2,1)} %ck_hbm.1, bf16[4,2048,128]{2,1,0:T(8,128)(2,1)} %cv_hbm.1, bf16[512,8192]{1,0:T(8,128)(2,1)} %w_hbm.1, ...), custom_call_target="tpu_custom_call" | custom-call | tf_op jit(solution)/shard_map/attend/pallas_call | solution.py:414
  57.1 0.8 %copy.10 = bf16[512,512]{1,0:T(8,128)(2,1)} copy(bf16[512,512]{1,0:T(8,128)(2,1)S(1)} %attend.1) | data formatting | bytes 1048576

commit v3 on v2

v3 whole, which is shorter than its diff:
```python
import jax
import jax.numpy as jnp
from jax import lax
from jax.experimental import pallas as pl
from jax.experimental.pallas import tpu as pltpu
from jax.sharding import PartitionSpec as P

D = 8192
HD = 128
SPAN = 128
SEQS = 4
HALF = 2048
COLS = 512
EPSILON = 1e-05
SCALE = HD**-0.5 * 1.4426950408889634

MESH = pl.DeviceIdType.MESH
F32 = jnp.float32
BF16 = jnp.bfloat16

ORDER = ((2, 1), (2, 0), (1, 1), (3, 0), (3, 1), (0, 1), (1, 0), (0, 0))
SLOT = {key: slot for slot, key in enumerate(ORDER)}
WIDE = COLS // 2
TALL = SPAN // 2
LAST = SEQS - 1
GROUPS = ((0, 1, 2, 3), (4, 5, 6, 7))
HEADS = 2
ROWS = HEADS * SPAN
CHUNKS = 4 // HEADS


def dot_t(a, b):
    return lax.dot_general(a, b, (((1,), (1,)), ((), ())), preferred_element_type=F32)


def dot(a, b):
    return jnp.dot(a, b, preferred_element_type=F32)


def with_ones(v, axis=1):
    return jnp.concatenate([v, jnp.ones_like(v)], axis=axis)


def kernel(
    q_hbm, nk_hbm, nv_hbm, ck_hbm, cv_hbm, w_hbm, res_hbm, gain_ref, out_ref,
    q_v, kown, vown, koth, voth, nk, nv, wown, wsend, m_ref, acc_ref, aown, psend, precv,
    pbuf, fbuf, xbuf, r1, r2, rx, rxx, cbuf, gbuf, q1, q2, q3,
    hid, res_v, ss, ssr,
    load_sem, kvl_sem, wl_sem, sent, kv_recv, nkv_recv, p_recv,
    r1_recv, r2_recv, x_recv, xx_recv, q1_recv, q2_recv, q3_recv, ss_recv,
):
    me = lax.axis_index("tp")
    core = lax.rem(me, 2)
    xh = lax.rem(lax.div(me, 2), 2)
    y = lax.div(me, 4)
    half = pl.ds(pl.multiple_of(core * (HD // 2), HD // 2), HD // 2)

    def peer(dy, dx, dc):
        py = lax.rem(y + dy, 4)
        px = lax.rem(xh + dx, 2)
        pc = lax.rem(core + dc, 2)
        return (py * 2 + px) * 2 + pc

    partner = peer(0, 0, 1)
    up, down, far, across = peer(1, 0, 0), peer(3, 0, 0), peer(2, 0, 0), peer(0, 1, 0)

    def remote(src, dst, send, recv, dev):
        return pltpu.make_async_remote_copy(
            src_ref=src, dst_ref=dst, send_sem=send, recv_sem=recv,
            device_id={"tp": dev}, device_id_type=MESH,
        )

    def kv_local(s):
        return (
            pltpu.make_async_copy(ck_hbm.at[s], kown.at[s], kvl_sem.at[s, 0]),
            pltpu.make_async_copy(cv_hbm.at[s], vown.at[s], kvl_sem.at[s, 1]),
        )

    def kv_remote(s):
        return (
            remote(kown.at[s], koth.at[s], sent.at[0], kv_recv.at[s, 0], partner),
            remote(vown.at[s], voth.at[s], sent.at[1], kv_recv.at[s, 1], partner),
        )

    def columns(slot, dc):
        dy, dx = ORDER[slot]
        start = peer(dy, dx, dc) * COLS
        return w_hbm.at[:, pl.ds(pl.multiple_of(start, COLS), COLS)]

    def w_local(slot):
        return pltpu.make_async_copy(columns(slot, 0), wown.at[slot], wl_sem.at[0])

    def w_staged(slot):
        return pltpu.make_async_copy(columns(slot, 1), wsend.at[slot], wl_sem.at[1])

    def nkv_remote():
        return (
            remote(nk.at[half], nk.at[half], sent.at[2], nkv_recv.at[0], partner),
            remote(nv.at[half], nv.at[half], sent.at[3], nkv_recv.at[1], partner),
        )

    def wait_bytes(ref, sem):
        pltpu.make_async_copy(ref, ref, sem).wait()

    def share_remote(s, slot):
        return remote(
            psend.at[s, slot], precv.at[s, slot], sent.at[4], p_recv.at[s, slot // 4], partner
        )

    def first_remote(s):
        return (
            remote(pbuf.at[s, SLOT[2, 0], 0], r1.at[s, 0], sent.at[5], r1_recv.at[s, 0], up),
            remote(pbuf.at[s, SLOT[2, 1], 0], r1.at[s, 1], sent.at[5], r1_recv.at[s, 1], down),
        )

    def direct_remote(s):
        return (
            remote(pbuf.at[s, SLOT[1, 1], 0], r2.at[s, 1], sent.at[5], r2_recv.at[s, 1], up),
            remote(pbuf.at[s, SLOT[3, 0], 0], r2.at[s, 2], sent.at[5], r2_recv.at[s, 2], down),
        )

    def forward_remote(s):
        return (
            remote(fbuf.at[s, 0], r2.at[s, 0], sent.at[6], r2_recv.at[s, 0], up),
            remote(fbuf.at[s, 1], r2.at[s, 3], sent.at[6], r2_recv.at[s, 3], down),
        )

    def x_remote(s):
        return remote(xbuf.at[s], rx.at[s], sent.at[7], x_recv.at[s], across)

    def x_first_remote(s, dy):
        return remote(
            pbuf.at[s, SLOT[dy, 1], 1], rxx.at[s, dy], sent.at[5], xx_recv.at[s, dy], across
        )

    def y_last_remote():
        return tuple(
            remote(cbuf.at[LAST, i], q3.at[i], sent.at[8], q3_recv.at[i], dev)
            for i, dev in enumerate((far, up, down))
        )

    def tall(ref, s, i, low):
        return ref.at[s, i, pl.ds(low * TALL, TALL)]

    def y_first_remote(s):
        return (
            remote(tall(cbuf, s, 0, 0), q1.at[s, 0], sent.at[10], q1_recv.at[s, 0], up),
            remote(tall(cbuf, s, 0, 1), q1.at[s, 1], sent.at[10], q1_recv.at[s, 1], down),
        )

    def y_direct_remote(s):
        return (
            remote(tall(cbuf, s, 1, 1), tall(q2, s, 0, 1), sent.at[11], q2_recv.at[s, 1], up),
            remote(tall(cbuf, s, 2, 0), tall(q2, s, 1, 0), sent.at[11], q2_recv.at[s, 2], down),
        )

    def y_forward_remote(s):
        return (
            remote(gbuf.at[s, 0], tall(q2, s, 0, 0), sent.at[12], q2_recv.at[s, 0], up),
            remote(gbuf.at[s, 1], tall(q2, s, 1, 1), sent.at[12], q2_recv.at[s, 3], down),
        )

    others = [(dy, dx, dc) for dy in range(4) for dx in range(2) for dc in range(2)][1:]

    def square_remote(i):
        return remote(ss, ssr.at[i], sent.at[9], ss_recv, peer(*others[i]))

    load = (
        pltpu.make_async_copy(q_hbm, q_v, load_sem.at[0]),
        pltpu.make_async_copy(nk_hbm, nk.at[half], load_sem.at[1]),
        pltpu.make_async_copy(nv_hbm, nv.at[half], load_sem.at[2]),
        pltpu.make_async_copy(res_hbm, res_v, load_sem.at[3]),
    )

    barrier = pltpu.get_barrier_semaphore()
    for dev in (partner, up, down, far, across):
        pl.semaphore_signal(barrier, inc=1, device_id={"tp": dev}, device_id_type=MESH)
    first_load = kv_local(0) + load[1:3] + load[:1]
    for copy in first_load:
        copy.start()
    for copy in first_load:
        copy.wait()
    for slot in range(8):
        w_staged(slot).start()
    pl.semaphore_wait(barrier, 5)

    for pair in zip(kv_remote(0), nkv_remote()):
        for copy in pair:
            copy.start()
    for copy in kv_local(1):
        copy.start()
    for slot in range(8):
        w_local(slot).start()
    for s in range(2, SEQS):
        for copy in kv_local(s):
            copy.start()
    load[3].start()

    def rows_of(s, chunk):
        part = q_v[pl.ds(pl.multiple_of(s * SPAN, SPAN), SPAN), :]
        heads = range(chunk * HEADS, (chunk + 1) * HEADS)
        return jnp.concatenate([part[:, h * HD : (h + 1) * HD] for h in heads], axis=0)

    def chunk_rows(chunk):
        return slice(chunk * ROWS, (chunk + 1) * ROWS)

    def own_half(s):
        upcoming = dot_t(rows_of(s, 0), kown[s])
        for chunk in range(CHUNKS):
            scores = upcoming
            if chunk + 1 < CHUNKS:
                upcoming = dot_t(rows_of(s, chunk + 1), kown[s])
            rows = chunk_rows(chunk)
            peak = jnp.max(scores, axis=1, keepdims=True)
            weights = jnp.exp2((scores - peak) * SCALE).astype(BF16)
            acc_ref[rows, :] = dot(weights, with_ones(vown[s]))
            m_ref[rows, :] = jnp.broadcast_to(peak, (ROWS, HD))

    def other_half(s):
        kv_remote(s)[0].wait_recv()
        tokens = pl.ds(pl.multiple_of(s * SPAN, SPAN), SPAN)

        def scores_of(chunk):
            q = rows_of(s, chunk)
            recent = dot(q, nk[:, tokens])
            row = lax.rem(lax.broadcasted_iota(jnp.int32, recent.shape, 0), SPAN)
            col = lax.broadcasted_iota(jnp.int32, recent.shape, 1)
            return dot_t(q, koth[s]), jnp.where(row >= col, recent, -jnp.inf)

        upcoming = scores_of(0)
        for chunk in range(CHUNKS):
            scores, recent = upcoming
            if chunk + 1 < CHUNKS:
                upcoming = scores_of(chunk + 1)
            rows = chunk_rows(chunk)
            old = m_ref[rows, :1]
            peak = jnp.maximum(
                jnp.max(scores, axis=1, keepdims=True), jnp.max(recent, axis=1, keepdims=True)
            )
            peak = jnp.maximum(peak, old)
            weights = jnp.exp2((scores - peak) * SCALE).astype(BF16)
            recent_weights = jnp.exp2((recent - peak) * SCALE).astype(BF16)
            mixed = acc_ref[rows, :] * jnp.exp2((old - peak) * SCALE)
            if chunk == 0:
                kv_remote(s)[1].wait_recv()
            mixed = mixed + dot(weights, with_ones(voth[s]))
            mixed = mixed + dot_t(recent_weights, with_ones(nv[:, tokens], 0))
            result = (mixed[:, :HD] / mixed[:, HD:]).astype(BF16)
            for i in range(HEADS):
                h = chunk * HEADS + i
                aown[s, :, h * HD : (h + 1) * HD] = result[i * SPAN : (i + 1) * SPAN, :]

    def wide(ref):
        return ref.astype(F32)

    def share(s):
        for group in GROUPS:
            for slot in group:
                psend[s, slot] = dot(aown[s], wsend[slot]).astype(BF16)
            for slot in group:
                share_remote(s, slot).start()

    def project(s):
        for group in GROUPS:
            blocks = [dot(aown[s], wown[slot]) for slot in group]
            wait_bytes(precv.at[s, pl.ds(group[0], 4)], p_recv.at[s, group[0] // 4])
            for slot, block in zip(group, blocks):
                block = (block + wide(precv[s, slot])).astype(BF16)
                pbuf[s, slot, 0] = block[:, :WIDE]
                pbuf[s, slot, 1] = block[:, WIDE:]
            for slot in group:
                dy, dx = ORDER[slot]
                if dx == 1:
                    x_first_remote(s, dy).start()
                if dy == 2:
                    first_remote(s)[dx].start()
                elif (dy, dx) == (1, 1):
                    direct_remote(s)[0].start()
                elif (dy, dx) == (3, 0):
                    direct_remote(s)[1].start()

    def forward(s):
        for i, slot in enumerate((SLOT[1, 0], SLOT[3, 1])):
            first_remote(s)[i].wait_recv()
            fbuf[s, i] = (wide(r1[s, i]) + wide(pbuf[s, slot, 0])).astype(BF16)
            forward_remote(s)[i].start()

    def send_across(s):
        direct_remote(s)[0].wait_recv()
        forward_remote(s)[1].wait_recv()
        total = wide(pbuf[s, SLOT[0, 1], 0]) + wide(r2[s, 1]) + wide(r2[s, 3])
        xbuf[s] = total.astype(BF16)
        x_remote(s).start()

    def sum_across(s):
        for i, dy in enumerate((2, 1, 3)):
            x_first_remote(s, dy).wait_recv()
            cbuf[s, i] = (wide(pbuf[s, SLOT[dy, 0], 1]) + wide(rxx[s, dy])).astype(BF16)
            if isinstance(s, int):
                y_last_remote()[i].start()
            elif i == 0:
                for copy in y_first_remote(s):
                    copy.start()
            else:
                y_direct_remote(s)[i - 1].start()

    def y_forward(s):
        for i in range(2):
            y_first_remote(s)[i].wait_recv()
            kept = wide(cbuf[s, 1 + i, i * TALL : (i + 1) * TALL, :])
            gbuf[s, i] = (wide(q1[s, i]) + kept).astype(BF16)
            y_forward_remote(s)[i].start()

    def finish(s):
        tokens = pl.ds(pl.multiple_of(s * SPAN, SPAN), SPAN)
        x_first_remote(s, 0).wait_recv()
        right = wide(pbuf[s, SLOT[0, 0], 1]) + wide(rxx[s, 0])
        if s == LAST:
            for i, copy in enumerate(y_last_remote()):
                copy.wait_recv()
                right = right + wide(q3[i])
        else:
            for copy in y_direct_remote(s) + y_forward_remote(s):
                copy.wait_recv()
            right = right + wide(q2[s, 0]) + wide(q2[s, 1])
        right = right + wide(res_v[tokens, WIDE:])
        hid[s, :, WIDE:] = right
        direct_remote(s)[1].wait_recv()
        forward_remote(s)[0].wait_recv()
        left = wide(pbuf[s, SLOT[0, 0], 0]) + wide(r2[s, 0]) + wide(r2[s, 2])
        left = left + wide(res_v[tokens, :WIDE])
        x_remote(s).wait_recv()
        left = left + wide(rx[s])
        hid[s, :, :WIDE] = left
        column = jnp.sum(left * left + right * right, axis=1, keepdims=True)
        ss[s : s + 1, :] = jnp.transpose(jnp.broadcast_to(column, (SPAN, SPAN)))[:1, :]

    own_half(0)
    for copy in kv_local(1):
        copy.wait()
    for copy in kv_remote(1):
        copy.start()
    for copy in nkv_remote():
        copy.wait_recv()

    def sequence(s, carry):
        other_half(s)

        @pl.when(s == 0)
        def _():
            wait_bytes(wown, wl_sem.at[0])
            wait_bytes(wsend, wl_sem.at[1])

        share(s)

        @pl.when(s < SEQS - 2)
        def _():
            for copy in kv_local(s + 2):
                copy.wait()
            for copy in kv_remote(s + 2):
                copy.start()

        @pl.when(s >= 1)
        def _():
            forward(s - 1)

        @pl.when(s >= 2)
        def _():
            send_across(s - 2)
            y_forward(s - 2)

        @pl.when((s >= 1) & (s < SEQS - 1))
        def _():
            own_half(s + 1)

        project(s)

        @pl.when(s == 0)
        def _():
            own_half(1)

        @pl.when(s >= 1)
        def _():
            sum_across(s - 1)

        return carry

    lax.fori_loop(0, SEQS, sequence, 0)

    load[3].wait()
    ss[...] = jnp.zeros_like(ss)
    finish(0)
    forward(LAST)
    send_across(LAST - 1)
    y_forward(LAST - 1)
    finish(1)
    sum_across(SEQS - 1)
    send_across(SEQS - 1)
    finish(2)
    finish(3)

    for i in range(15):
        square_remote(i).start()

    sources = (
        kown, vown, nk.at[half], nv.at[half], psend, pbuf.at[:, pl.ds(0, 4)], fbuf, xbuf,
        cbuf.at[LAST], ssr, q1, q1, gbuf,
    )
    for i, ref in enumerate(sources):
        if ref is not ssr:
            wait_bytes(ref, sent.at[i])

    lines = gain_ref[...].astype(F32)
    gain = jnp.concatenate([lines[i : i + 1, :] for i in range(4)], axis=1)
    wait_bytes(ssr, ss_recv)
    squares = ss[...]
    for i in range(15):
        squares = squares + ssr[i]
    rows = lax.rsqrt(squares * (1.0 / D) + EPSILON)
    for s in range(SEQS):
        column = jnp.transpose(jnp.broadcast_to(rows[s : s + 1, :], (SPAN, SPAN)))[:, :1]
        out_ref[s * SPAN : (s + 1) * SPAN, :] = (hid[s] * column * gain).astype(BF16)
    wait_bytes(ssr, sent.at[9])


def per_device(queries, new_keys, new_values, cache_keys, cache_values, out_weight, residual, gain):
    any_spec = pl.BlockSpec(memory_space=pl.ANY)
    vmem_spec = pl.BlockSpec(memory_space=pltpu.VMEM)
    dma = pltpu.SemaphoreType.DMA
    block = (SPAN, WIDE)
    return pl.pallas_call(
        kernel,
        name="attend",
        out_shape=pltpu.VMEM((SEQS * SPAN, COLS), BF16),
        in_specs=[any_spec] * 7 + [vmem_spec],
        out_specs=vmem_spec,
        scratch_shapes=[
            pltpu.VMEM((SEQS * SPAN, 4 * HD), BF16),
            *[pltpu.VMEM((SEQS, HALF, HD), BF16)] * 4,
            *[pltpu.VMEM((HD, SEQS * SPAN), BF16)] * 2,
            *[pltpu.VMEM((8, COLS, COLS), BF16)] * 2,
            pltpu.VMEM((4 * SPAN, HD), F32),
            pltpu.VMEM((4 * SPAN, 2 * HD), F32),
            pltpu.VMEM((SEQS, SPAN, COLS), BF16),
            *[pltpu.VMEM((SEQS, 8, SPAN, COLS), BF16)] * 2,
            pltpu.VMEM((SEQS, 8, 2, *block), BF16),
            pltpu.VMEM((SEQS, 2, *block), BF16),
            pltpu.VMEM((SEQS, *block), BF16),
            pltpu.VMEM((SEQS, 2, *block), BF16),
            pltpu.VMEM((SEQS, 4, *block), BF16),
            pltpu.VMEM((SEQS, *block), BF16),
            pltpu.VMEM((SEQS, 4, *block), BF16),
            pltpu.VMEM((SEQS, 3, *block), BF16),
            *[pltpu.VMEM((LAST, 2, TALL, WIDE), BF16)] * 2,
            pltpu.VMEM((LAST, 2, *block), BF16),
            pltpu.VMEM((3, *block), BF16),
            pltpu.VMEM((SEQS, SPAN, COLS), F32),
            pltpu.VMEM((SEQS * SPAN, COLS), BF16),
            pltpu.VMEM((8, SPAN), F32),
            pltpu.VMEM((15, 8, SPAN), F32),
            dma((4,)), dma((SEQS, 2)), dma((2,)), dma((13,)), dma((SEQS, 2)), dma((2,)),
            dma((SEQS, 2)), dma((SEQS, 2)), dma((SEQS, 4)), dma((SEQS,)), dma((SEQS, 4)),
            dma((LAST, 2)), dma((LAST, 4)), dma((3,)), dma,
        ],
        compiler_params=pltpu.CompilerParams(
            collective_id=0, has_side_effects=True, vmem_limit_bytes=60 * 2**20
        ),
    )(
        queries, new_keys.T, new_values.T, cache_keys, cache_values, out_weight, residual,
        gain.reshape(4, 128),
    )


def solution(mesh):
    in_specs = (
        P("dp", "tp"),
        P("dp", "tp"),
        P("dp", "tp"),
        P("dp", "tp", None),
        P("dp", "tp", None),
        P("tp", None),
        P("dp", "tp"),
        P("tp"),
    )
    return jax.shard_map(
        per_device, mesh=mesh, in_specs=in_specs, out_specs=P("dp", "tp"), check_vma=False
    )
```

time: 58 us -> 55.1 us (0.950); the launches traced: 57.9 us -> 54.2 us
  Pallas kernels: 57.1 us -> 53.4 us
    pallas_call x1, Pallas kernels: 57.1 us -> 53.4 us  [per_device(): pl.pallas_call(kernel, name='attend', out_shape=pltpu.VMEM((SEQS * SPAN,...]
where the time goes in v3:
time: 55.1 us; the launch traced here: 54.2 us
  Pallas kernels  53.4 us (97%)
  local copies, waits for them, and re-layouts  0.8 us (1%)
    pallas_call x1, Pallas kernels, per_device(): pl.pallas_call(kernel, name='attend', out_shape=pltpu.VMEM((SEQS * SPAN,...  53.4 us

profile of v3, /device:TPU:1, one launch (start us, length us, event | category | flops | bytes accessed | tf_op | source)
XLA Modules:
  0.0 54.2 jit_solution(5096009798854419205)
XLA Ops:
  0.0 53.4 %attend.1 = bf16[512,512]{1,0:T(8,128)(2,1)S(1)} custom-call(bf16[512,512]{1,0:T(8,128)(2,1)} %q_hbm.1, bf16[64,512]{1,0:T(8,128)(2,1)} %bitcast.3, bf16[64,512]{1,0:T(8,128)(2,1)} %bitcast.4, bf16[4,2048,128]{2,1,0:T(8,128)(2,1)} %ck_hbm.1, bf16[4,2048,128]{2,1,0:T(8,128)(2,1)} %cv_hbm.1, bf16[512,8192]{1,0:T(8,128)(2,1)} %w_hbm.1, ...), custom_call_target="tpu_custom_call" | custom-call | tf_op jit(solution)/shard_map/attend/pallas_call | solution.py:431
  53.4 0.8 %copy.10 = bf16[512,512]{1,0:T(8,128)(2,1)} copy(bf16[512,512]{1,0:T(8,128)(2,1)S(1)} %attend.1) | data formatting | bytes 1048576

commit v4 on v3

--- a/solution.py
+++ b/solution.py
@@ -292,11 +292,11 @@
         xbuf[s] = total.astype(BF16)
         x_remote(s).start()
 
-    def sum_across(s):
+    def sum_across(s, last=False):
         for i, dy in enumerate((2, 1, 3)):
             x_first_remote(s, dy).wait_recv()
             cbuf[s, i] = (wide(pbuf[s, SLOT[dy, 0], 1]) + wide(rxx[s, dy])).astype(BF16)
-            if isinstance(s, int):
+            if last:
                 y_last_remote()[i].start()
             elif i == 0:
                 for copy in y_first_remote(s):
@@ -360,6 +360,10 @@
             for copy in kv_remote(s + 2):
                 copy.start()
 
+        @pl.when((s >= 1) & (s < SEQS - 1))
+        def _():
+            own_half(s + 1)
+
         @pl.when(s >= 1)
         def _():
             forward(s - 1)
@@ -367,21 +371,20 @@
         @pl.when(s >= 2)
         def _():
             send_across(s - 2)
+
+        project(s)
+
+        @pl.when(s == 0)
+        def _():
+            own_half(1)
+
+        @pl.when(s >= 1)
+        def _():
+            sum_across(s - 1)
+
+        @pl.when(s >= 2)
+        def _():
             y_forward(s - 2)
-
-        @pl.when((s >= 1) & (s < SEQS - 1))
-        def _():
-            own_half(s + 1)
-
-        project(s)
-
-        @pl.when(s == 0)
-        def _():
-            own_half(1)
-
-        @pl.when(s >= 1)
-        def _():
-            sum_across(s - 1)
 
         return carry
 
@@ -390,12 +393,12 @@
     load[3].wait()
     ss[...] = jnp.zeros_like(ss)
     finish(0)
-    forward(LAST)
-    send_across(LAST - 1)
-    y_forward(LAST - 1)
+    forward(3)
+    send_across(2)
+    y_forward(2)
     finish(1)
-    sum_across(SEQS - 1)
-    send_across(SEQS - 1)
+    sum_across(LAST, last=True)
+    send_across(3)
     finish(2)
     finish(3)
 

time: 55.1 us -> 53.1 us (0.964); the launches traced: 54.2 us -> 52.9 us
  Pallas kernels: 53.4 us -> 52.1 us
    pallas_call x1, Pallas kernels: 53.4 us -> 52.1 us  [per_device(): pl.pallas_call(kernel, name='attend', out_shape=pltpu.VMEM((SEQS * SPAN,...]
where the time goes in v4:
time: 53.1 us; the launch traced here: 52.9 us
  Pallas kernels  52.1 us (98%)
  local copies, waits for them, and re-layouts  0.8 us (2%)
    pallas_call x1, Pallas kernels, per_device(): pl.pallas_call(kernel, name='attend', out_shape=pltpu.VMEM((SEQS * SPAN,...  52.1 us

profile of v4, /device:TPU:1, one launch (start us, length us, event | category | flops | bytes accessed | tf_op | source)
XLA Modules:
  0.0 52.9 jit_solution(12764145128329252679)
XLA Ops:
  0.0 52.1 %attend.1 = bf16[512,512]{1,0:T(8,128)(2,1)S(1)} custom-call(bf16[512,512]{1,0:T(8,128)(2,1)} %q_hbm.1, bf16[64,512]{1,0:T(8,128)(2,1)} %bitcast.3, bf16[64,512]{1,0:T(8,128)(2,1)} %bitcast.4, bf16[4,2048,128]{2,1,0:T(8,128)(2,1)} %ck_hbm.1, bf16[4,2048,128]{2,1,0:T(8,128)(2,1)} %cv_hbm.1, bf16[512,8192]{1,0:T(8,128)(2,1)} %w_hbm.1, ...), custom_call_target="tpu_custom_call" | custom-call | tf_op jit(solution)/shard_map/attend/pallas_call | solution.py:434
  52.2 0.8 %copy.10 = bf16[512,512]{1,0:T(8,128)(2,1)} copy(bf16[512,512]{1,0:T(8,128)(2,1)S(1)} %attend.1) | data formatting | bytes 1048576

commit v5 on v4

--- a/solution.py
+++ b/solution.py
@@ -378,13 +378,13 @@
         def _():
             own_half(1)
 
+        @pl.when(s >= 2)
+        def _():
+            y_forward(s - 2)
+
         @pl.when(s >= 1)
         def _():
             sum_across(s - 1)
-
-        @pl.when(s >= 2)
-        def _():
-            y_forward(s - 2)
 
         return carry
 

time: 53.1 us -> 52.8 us (level)
  no operation moved by 1% of the time
where the time goes in v5:
time: 52.8 us; the launch traced here: 52.7 us
  Pallas kernels  51.9 us (98%)
  local copies, waits for them, and re-layouts  0.8 us (2%)
    pallas_call x1, Pallas kernels, per_device(): pl.pallas_call(kernel, name='attend', out_shape=pltpu.VMEM((SEQS * SPAN,...  51.9 us

profile of v5, /device:TPU:1, one launch (start us, length us, event | category | flops | bytes accessed | tf_op | source)
XLA Modules:
  0.0 52.7 jit_solution(17924688037433146349)
XLA Ops:
  0.0 51.9 %attend.1 = bf16[512,512]{1,0:T(8,128)(2,1)S(1)} custom-call(bf16[512,512]{1,0:T(8,128)(2,1)} %q_hbm.1, bf16[64,512]{1,0:T(8,128)(2,1)} %bitcast.3, bf16[64,512]{1,0:T(8,128)(2,1)} %bitcast.4, bf16[4,2048,128]{2,1,0:T(8,128)(2,1)} %ck_hbm.1, bf16[4,2048,128]{2,1,0:T(8,128)(2,1)} %cv_hbm.1, bf16[512,8192]{1,0:T(8,128)(2,1)} %w_hbm.1, ...), custom_call_target="tpu_custom_call" | custom-call | tf_op jit(solution)/shard_map/attend/pallas_call | solution.py:434
  51.9 0.8 %copy.10 = bf16[512,512]{1,0:T(8,128)(2,1)} copy(bf16[512,512]{1,0:T(8,128)(2,1)S(1)} %attend.1) | data formatting | bytes 1048576

commit v6 on v4

--- a/solution.py
+++ b/solution.py
@@ -160,7 +160,7 @@
             remote(gbuf.at[s, 1], tall(q2, s, 1, 1), sent.at[12], q2_recv.at[s, 3], down),
         )
 
-    others = [(dy, dx, dc) for dy in range(4) for dx in range(2) for dc in range(2)][1:]
+    others = [(dy, dx, dc) for dy in range(4) for dx in range(2) for dc in range(2)][:0:-1]
 
     def square_remote(i):
         return remote(ss, ssr.at[i], sent.at[9], ss_recv, peer(*others[i]))
@@ -184,9 +184,8 @@
         w_staged(slot).start()
     pl.semaphore_wait(barrier, 5)
 
-    for pair in zip(kv_remote(0), nkv_remote()):
-        for copy in pair:
-            copy.start()
+    for copy in kv_remote(0)[:1] + nkv_remote() + kv_remote(0)[1:]:
+        copy.start()
     for copy in kv_local(1):
         copy.start()
     for slot in range(8):

time: 53.1 us -> 52.4 us (0.987)
  Pallas kernels: 52.1 us -> 51.5 us
    pallas_call x1, Pallas kernels: 52.1 us -> 51.5 us  [per_device(): pl.pallas_call(kernel, name='attend', out_shape=pltpu.VMEM((SEQS * SPAN,...]
where the time goes in v6:
time: 52.4 us; the launch traced here: 52.3 us
  Pallas kernels  51.5 us (98%)
  local copies, waits for them, and re-layouts  0.8 us (2%)
    pallas_call x1, Pallas kernels, per_device(): pl.pallas_call(kernel, name='attend', out_shape=pltpu.VMEM((SEQS * SPAN,...  51.5 us

profile of v6, /device:TPU:1, one launch (start us, length us, event | category | flops | bytes accessed | tf_op | source)
XLA Modules:
  0.0 52.3 jit_solution(16919638400484073929)
XLA Ops:
  0.0 51.5 %attend.1 = bf16[512,512]{1,0:T(8,128)(2,1)S(1)} custom-call(bf16[512,512]{1,0:T(8,128)(2,1)} %q_hbm.1, bf16[64,512]{1,0:T(8,128)(2,1)} %bitcast.3, bf16[64,512]{1,0:T(8,128)(2,1)} %bitcast.4, bf16[4,2048,128]{2,1,0:T(8,128)(2,1)} %ck_hbm.1, bf16[4,2048,128]{2,1,0:T(8,128)(2,1)} %cv_hbm.1, bf16[512,8192]{1,0:T(8,128)(2,1)} %w_hbm.1, ...), custom_call_target="tpu_custom_call" | custom-call | tf_op jit(solution)/shard_map/attend/pallas_call | solution.py:433
  51.5 0.8 %copy.10 = bf16[512,512]{1,0:T(8,128)(2,1)} copy(bf16[512,512]{1,0:T(8,128)(2,1)S(1)} %attend.1) | data formatting | bytes 1048576
